TPU v7x, 32 devices: a whole 2x2x4 slice. The times are simulated.
32 devices in a mesh: groups: 2 (over y), rows: 4 (over z), cols: 2 (over x), sub: 2 (over core).
Axes of the slice: x: 2, y: 2, z: 4, core: 2. Of those that a mesh axis runs over, the one named last changes fastest.
Arguments:
- stored_vectors: bfloat16 [3072, 8192], P(('cols', 'sub'), ('groups', 'rows')), parts along dimension 1, may hold values from -0.59765625 to 0.59765625
- previous_columns: bfloat16 [8192, 256], P(('groups', 'rows', 'cols', 'sub')), parts along dimension 0, may hold values from -3 to 3
- pivots: int32 [512], P('groups'), parts along dimension 0, may hold values from 0 to 4095, as said below
- diagonal: float32 [8192], P(('groups', 'rows', 'cols', 'sub')), parts along dimension 0, may hold values from 2 to 32
- ket_blocks: bfloat16 [128, 128, 256], P(('groups', 'rows', 'cols', 'sub')), parts along dimension 0, may hold values from -6 to 6
- shell_tags: int32 [128, 128], P(('groups', 'rows', 'cols', 'sub')), parts along dimension 0, may hold values from 0 to 3
- target_blocks: int32 [32, 4], P('groups'), parts along dimension 0, may hold values from 0 to 31, as said below
- block_counts: int32 [32], P('groups'), parts along dimension 0, may hold values from 0 to 4, as said below
- shell_norms: float32 [4], replicated, may hold values from 0.5 to 2
Outputs:
- new_vectors: bfloat16 [8192, 256], P(('groups', 'rows', 'cols', 'sub')), parts along dimension 0
- diag_out: float32 [8192], P(('groups', 'rows', 'cols', 'sub')), parts along dimension 0
- next_columns: bfloat16 [8192, 256], P(('groups', 'rows', 'cols', 'sub')), parts along dimension 0
There are 2 independent parts, one for each index of `groups`. A program takes and returns all parts, laid end to end along the dimension named above; an argument that names none is the same for every part. Nothing has to cross between parts.
Inputs may be any that keep to these rules, and one draw needn't show every extreme that they name: `pivots`: 256 distinct AO pairs. `target_blocks`: the used slots of all owners name every block of the 32 blocks exactly once; a used slot's block lies on a device with the owner's cols and sub indices (blocks g * 2 to g * 2 + 1 lie on the device of linear index g, rows slowest; owner o is the device of linear index o). At most 1 of one owner's used slots go to one device, and some owner reaches that in every draw. Entries of unused slots are arbitrary blocks. `block_counts`: some owner uses all 4 slots in every draw.
All inputs are finite; a program needn't handle non-finite values.
Results may differ from a plain program's by a relative error of at most 0.0004.
Values may be sent and summed in bfloat16 or wider, within the bound.
A program may use at most 64 MiB of HBM per device.

v0:
```python
import jax
import jax.numpy as jnp
from jax import lax
from jax.sharding import PartitionSpec as P


def slot_plan(row_targets, count, column_size, per_device):
    slot_count = row_targets.shape[0]
    slots = jnp.arange(slot_count, dtype=jnp.int32)
    valid = slots < count
    receiver = row_targets // (column_size * per_device)
    within = row_targets % per_device
    earlier = (
        (receiver[:, None] == receiver[None, :])
        & valid[:, None]
        & valid[None, :]
        & (slots[None, :] < slots[:, None])
    )
    ranking = jnp.sum(earlier.astype(jnp.int32), axis=1)
    return (valid, receiver, ranking, within)


def body(
    stored_vectors,
    previous_columns,
    pivots,
    diagonal,
    ket_blocks,
    shell_tags,
    target_blocks,
    block_counts,
    shell_norms,
):
    rows_here = previous_columns.shape[0]
    batch = previous_columns.shape[1]
    block_rows = ket_blocks.shape[1]
    slot_count = ket_blocks.shape[0]
    per_device = rows_here // block_rows
    band_rows = stored_vectors.shape[1]
    band_index = lax.axis_index("rows")
    device_index = lax.axis_index(("rows", "cols", "sub"))
    column_index = lax.axis_index(("cols", "sub"))
    column_size = lax.axis_size(("cols", "sub"))
    band_size = lax.axis_size("rows")
    peer_slots = (slot_count + band_size - 1) // band_size
    local_pivots = pivots - device_index * rows_here
    matches = jnp.arange(rows_here, dtype=jnp.int32)[:, None] == local_pivots[None, :]
    diag_terms = jnp.sum(jnp.where(matches, diagonal[:, None], jnp.float32(0.0)), axis=0)
    pivot_diag = lax.psum(diag_terms, ("rows", "cols", "sub"))
    band_pivots = pivots - band_index * band_rows
    inside = (band_pivots >= 0) & (band_pivots < band_rows)
    clamped = jnp.clip(band_pivots, 0, band_rows - 1)
    taken = jnp.take(stored_vectors, clamped, axis=1).astype(jnp.float32)
    picked = jnp.where(inside[None, :], taken, jnp.float32(0.0))
    pivot_rows = lax.psum(picked, "rows").astype(jnp.bfloat16)
    kinds = jnp.arange(shell_norms.shape[0], dtype=jnp.int32)
    factor = jnp.sum(
        jnp.where(shell_tags[..., None] == kinds, shell_norms, jnp.float32(0.0)), axis=-1
    )
    fresh = (ket_blocks.astype(jnp.float32) * factor[..., None]).astype(jnp.bfloat16)
    own_targets = lax.dynamic_index_in_dim(target_blocks, device_index, 0, keepdims=False)
    own_count = lax.dynamic_index_in_dim(block_counts, device_index, 0, keepdims=False)
    valid, receiver, ranking, within = slot_plan(own_targets, own_count, column_size, per_device)
    lines = jnp.arange(band_size * peer_slots, dtype=jnp.int32)[:, None]
    routing = (
        (lines // peer_slots == receiver[None, :])
        & (lines % peer_slots == ranking[None, :])
        & valid[None, :]
    ).astype(jnp.bfloat16)
    outgoing = jnp.dot(
        routing, fresh.reshape(slot_count, block_rows * batch), preferred_element_type=jnp.float32
    )
    outgoing = outgoing.astype(jnp.bfloat16).reshape(band_size, peer_slots, block_rows, batch)
    incoming = lax.all_to_all(outgoing, "rows", split_axis=0, concat_axis=0, tiled=True)
    sources = jnp.arange(band_size, dtype=jnp.int32) * column_size + column_index
    source_targets = jnp.take(target_blocks, sources, axis=0)
    source_counts = jnp.take(block_counts, sources, axis=0)
    plan_each = jax.vmap(
        lambda row_targets, count: slot_plan(row_targets, count, column_size, per_device)
    )
    source_valid, source_receiver, source_rank, source_within = plan_each(
        source_targets, source_counts
    )
    arriving = source_valid & (source_receiver == band_index)
    places = jnp.arange(per_device, dtype=jnp.int32)[:, None, None, None]
    peer_lines = jnp.arange(peer_slots, dtype=jnp.int32)[None, None, :, None]
    hits = (
        (source_within[None, :, None, :] == places)
        & (source_rank[None, :, None, :] == peer_lines)
        & arriving[None, :, None, :]
    )
    placement = (
        jnp.any(hits, axis=3).astype(jnp.bfloat16).reshape(per_device, band_size * peer_slots)
    )
    arranged = jnp.dot(
        placement,
        incoming.reshape(band_size * peer_slots, block_rows * batch),
        preferred_element_type=jnp.float32,
    )
    next_columns = arranged.astype(jnp.bfloat16).reshape(rows_here, batch)
    product = lax.psum_scatter(
        lax.dot_general(
            stored_vectors, pivot_rows, (((0,), (0,)), ((), ())), preferred_element_type=jnp.float32
        ),
        ("cols", "sub"),
        scatter_dimension=0,
        tiled=True,
    )
    residual_cols = previous_columns.astype(jnp.float32) - product
    scaled = residual_cols / jnp.sqrt(pivot_diag)[None, :]
    new_vectors = scaled.astype(jnp.bfloat16)
    diag_out = diagonal - jnp.sum(scaled * scaled, axis=1)
    return (new_vectors, diag_out, next_columns)


def solution(mesh):
    return jax.shard_map(
        body,
        mesh=mesh,
        in_specs=(
            P(("cols", "sub"), ("groups", "rows")),
            P(("groups", "rows", "cols", "sub"), None),
            P("groups"),
            P(("groups", "rows", "cols", "sub")),
            P(("groups", "rows", "cols", "sub"), None, None),
            P(("groups", "rows", "cols", "sub"), None),
            P("groups", None),
            P("groups"),
            P(),
        ),
        out_specs=(
            P(("groups", "rows", "cols", "sub"), None),
            P(("groups", "rows", "cols", "sub")),
            P(("groups", "rows", "cols", "sub"), None),
        ),
        check_vma=False,
    )
```

profile of v0, /device:TPU:0, one launch (start us, length us, event | category | flops | bytes accessed | tf_op | source)
XLA Modules:
  0.0 100.1 jit_solution(16816415105481037228)
XLA Ops:
  7.2 1.7 %copy.26 = bf16[768,1024]{0,1:T(8,128)(2,1)S(1)} copy(bf16[768,1024]{1,0:T(8,128)(2,1)} %param.9) | data formatting | bytes 3145728 | tf_op args[0]
  9.0 1.2 %gather_fusion = bf16[256,768]{1,0:T(8,128)(2,1)S(1)} fusion(bf16[768,1024]{0,1:T(8,128)(2,1)S(1)} %copy.26, s32[1024]{0:T(1024)S(1)} %pad_clamp_fusion.1), kind=kCustom, calls=%fused_computation | custom fusion | bytes 787456 | tf_op jit(solution)/shard_map/jit(_take)/gather | solution.py:53
  10.2 0.2 select_bitcast_fusion
  10.4 37.4 %all-reduce.1 = bf16[768,256]{0,1:T(8,128)(2,1)S(1)} all-reduce(f32[768,256]{0,1:T(8,128)S(1)} %select_bitcast_fusion), channel_id=1, replica_groups=mesh['groups'=2,'rows'=4,'cols'=2,'sub'=2] {'rows'}, use_global_device_ids=true, to_apply=%region_0.1 | all-reduce | flops 196608 | bytes 1179648 | tf_op jit(solution)/shard_map/psum | solution.py:55
  47.9 1.6 %convolution_bitcast_fusion = f32[1024,256]{0,1:T(8,128)} fusion(bf16[768,1024]{1,0:T(8,128)(2,1)S(1)} %copy-done.1, bf16[768,256]{0,1:T(8,128)(2,1)S(1)} %all-reduce.1), kind=kOutput, calls=%fused_computation.5 | convolution fusion | flops 402653184 | bytes 3014656 | tf_op jit(solution)/shard_map/dot_general | solution.py:102
  49.5 0.1 select_reduce_fusion.1
  49.6 0.1 fusion.1
  49.7 0.2 copy.30
  50.0 0.2 copy-done.4
  50.1 0.2 dynamic-slice_reduce_fusion
  50.3 0.6 dynamic_slice.9
  50.9 0.6 iota_compare_fusion.6
  51.6 0.2 convert_reduce_fusion.1
  51.8 0.3 convolution_convert_fusion
  52.1 0.7 copy.34
  52.8 3.4 %all-to-all-start = ((bf16[4,1,128,256]{3,2,1,0:T(8,128)(2,1)}), bf16[4,1,128,256]{3,2,1,0:T(8,128)(2,1)S(1)}, u32[]{:S(2)}, u32[]{:S(2)}) async-start(bf16[4,1,128,256]{3,2,1,0:T(8,128)(2,1)} %bitcast.26), calls=%async_computation.1 | async-start | bytes 524288 | tf_op jit(solution)/shard_map/all_to_all | solution.py:74
  56.2 0.1 copy.27
  56.3 0.6 gather_fusion.2
  57.0 0.6 gather_fusion.1
  57.6 0.1 compare_and_fusion
  57.6 0.2 convert_reduce_fusion
  57.9 0.1 select_reduce_fusion
  58.0 31.2 %psum.15 = f32[256]{0:T(256)S(1)} all-reduce(f32[256]{0:T(256)S(1)} %select_reduce_fusion), channel_id=1, replica_groups=mesh['groups'=2,'rows'=4,'cols'=2,'sub'=2] {'rows','cols','sub'}, use_global_device_ids=true, to_apply=%region_3.4 | all-reduce | flops 256 | bytes 2048 | tf_op jit(solution)/shard_map/psum | solution.py:49
  89.2 0.1 copy.25
  89.3 0.1 add_select_fusion.2
  89.4 0.2 fusion.4
  89.6 0.2 copy.32
  89.8 0.3 convolution_convert_fusion.1
  90.1 0.7 reshape.328
  90.8 1.1 %multiply_reduce_fusion = (f32[256]{0:T(256)S(1)}, bf16[256,256]{0,1:T(8,128)(2,1)S(1)}) fusion(f32[256]{0:T(256)S(1)} %sqrt.3, f32[256,256]{0,1:T(8,128)} %reduce-scatter.2.cloned.1.call-done, bf16[256,256]{0,1:T(8,128)(2,1)S(1)} %copy.25), kind=kLoop, calls=%fused_computation.11 | loop fusion | flops 392960 | bytes 526336 | tf_op jit(solution)/shard_map/reduce_sum | solution.py:112
  91.9 0.8 copy.29
  92.6 0.6 sub.35
  (32 shorter events, 0.2 us)
Async XLA Ops:
  7.2 83.6 %reduce-scatter.2.cloned.1.call-start = ((), (), s32[]{:S(2)}) async-start(), calls=%async_computation.2 | async-start | bytes 1310720 | tf_op jit(solution)/shard_map/reduce_scatter | solution.py:101
  7.2 1.7 %copy-start.6 = (s32[256]{0:T(256)S(1)}, s32[256]{0:T(256)}, u32[]{:S(2)}) copy-start(s32[256]{0:T(256)} %param.11) | copy-start | bytes 3076
  10.2 37.6 %copy-start.1 = (bf16[768,1024]{1,0:T(8,128)(2,1)S(1)}, bf16[768,1024]{1,0:T(8,128)(2,1)}, u32[]{:S(2)}) copy-start(bf16[768,1024]{1,0:T(8,128)(2,1)} %param.9) | copy-start | bytes 4718596
  47.8 1.6 %copy-start.7 = (s32[4,128]{1,0:T(4,128)S(1)}, s32[4,128]{1,0:T(4,128)}, u32[]{:S(2)}) copy-start(s32[4,128]{1,0:T(4,128)} %param.14) | copy-start | bytes 6148
  47.8 1.6 %copy-start.8 = (f32[4]{0:T(128)S(1)}, f32[4]{0:T(128)}, u32[]{:S(2)}) copy-start(f32[4]{0:T(128)} %param.17) | copy-start | bytes 52
  47.9 1.7 %copy-start.2 = (bf16[4,128,256]{2,1,0:T(8,128)(2,1)S(1)}, bf16[4,128,256]{2,1,0:T(8,128)(2,1)}, u32[]{:S(2)}) copy-start(bf16[4,128,256]{2,1,0:T(8,128)(2,1)} %param.13) | copy-start | bytes 786436
  49.4 0.7 copy-start.4
  49.4 0.9 copy-start
  49.6 8.3 %copy-start.5 = (f32[256]{0:T(256)S(1)}, f32[256]{0:T(256)}, u32[]{:S(2)}) copy-start(f32[256]{0:T(256)} %param.12) | copy-start | bytes 3076
  49.6 39.6 %copy-start.3 = (bf16[256,256]{1,0:T(8,128)(2,1)S(1)}, bf16[256,256]{1,0:T(8,128)(2,1)}, u32[]{:S(2)}) copy-start(bf16[256,256]{1,0:T(8,128)(2,1)} %param.10) | copy-start | bytes 393220
  52.8 36.7 %all-to-all-start = ((bf16[4,1,128,256]{3,2,1,0:T(8,128)(2,1)}), bf16[4,1,128,256]{3,2,1,0:T(8,128)(2,1)S(1)}, u32[]{:S(2)}, u32[]{:S(2)}) async-start(bf16[4,1,128,256]{3,2,1,0:T(8,128)(2,1)} %bitcast.26), calls=%async_computation.1 | async-start | bytes 524288 | tf_op jit(solution)/shard_map/all_to_all | solution.py:74
Sparse Core Ops, SparseCore 0:
  49.6 24.2 reduce-scatter.1
where the time goes:
time: 100 us
  blocking collectives  68.6 us (69%)
  between operations  14.3 us (14%)
  local copies, waits for them, and re-layouts  7.74 us (8%)
  other arithmetic  3.79 us (4%)
  starting transfers between devices  3.44 us (3%)
  matrix products  2.14 us (2%)
    psum x1, blocking collectives, body(): pivot_rows = lax.psum(picked, 'rows').astype(jnp.bfloat16)  37.4 us
    psum x1, blocking collectives, body(): pivot_diag = lax.psum(diag_terms, ('rows', 'cols', 'sub'))  31.2 us
    unnamed x25, local copies, waits for them, and re-layouts  4.02 us
    all_to_all x1, starting transfers between devices, body(): lax.all_to_all(outgoing, 'rows', split_axis=0, concat_axis=0, tiled=True)  3.4 us
  transfers between devices with their start and end apart: 2, of which 0 were waited for; matrix products, arithmetic and copies ran while one was open for 6% of the time, Pallas kernels for 0%

commit v1 on v0

v1 whole, which is shorter than its diff:
```python
import functools

import jax
import jax.numpy as jnp
from jax import lax
from jax.experimental import pallas as pl
from jax.experimental.pallas import tpu as pltpu
from jax.sharding import PartitionSpec as P

MESH = pl.DeviceIdType.MESH
LANES = 128


def column_of(row):
    return jnp.transpose(jnp.broadcast_to(row, (LANES, row.shape[1])))


def kernel(
    sizes,
    vec_hbm, prev_hbm, piv_ref, diag_ref, ket_hbm, tags_ref, targets_ref, counts_ref, norms_ref,
    new_ref, diag_out_ref, next_ref,
    vec, prev, ket, hot, own, fwd_r, fwd_l, from_l, from_r,
    pivot_t, prev_t, sub_out, sub_in, mine, col_out, col_in, scaled_t,
    stage, landed, pd_z, pd_s, pd_c, pd_own_s, pd_own_c,
    load_sem, zr_send, zl_send, l_recv, r_recv, sub_send, sub_recv, col_send, col_recv,
    ket_send, ket_recv, pdz_send, pdz_recv, pds_send, pds_recv, pdc_send, pdc_recv,
):
    n_rows, n_cols, n_sub, hop_lead = sizes
    z, x, s = lax.axis_index("rows"), lax.axis_index("cols"), lax.axis_index("sub")
    column_size = n_cols * n_sub
    column = x * n_sub + s
    device = z * column_size + column
    slot_count, block_rows, batch = ket_hbm.shape
    rows_here = prev_hbm.shape[0]
    per_device = rows_here // block_rows
    width, band_rows = vec_hbm.shape
    z_chunks, z_rows = own.shape[0], own.shape[1]
    m_chunks, m_rows = mine.shape[0], mine.shape[1]
    per_m = m_rows // z_rows

    load_ket = pltpu.make_async_copy(ket_hbm, ket, load_sem.at[0])
    load_vec = pltpu.make_async_copy(vec_hbm, vec, load_sem.at[1])
    load_prev = pltpu.make_async_copy(prev_hbm, prev, load_sem.at[2])
    load_ket.start()
    load_vec.start()
    load_prev.start()

    barrier = pltpu.get_barrier_semaphore()
    for name, here, count in (("rows", z, n_rows), ("cols", x, n_cols), ("sub", s, n_sub)):
        for d in range(1, count):
            pl.semaphore_signal(
                barrier, inc=1, device_id={name: lax.rem(here + d, count)}, device_id_type=MESH
            )

    piv_col = column_of(piv_ref[...].astype(jnp.float32)).astype(jnp.int32) - z * band_rows
    lane = lax.broadcasted_iota(jnp.int32, (batch, LANES), 1)
    for t in range(band_rows // LANES):
        hot[:, t * LANES:(t + 1) * LANES] = (piv_col == lane + t * LANES).astype(
            jnp.float32).astype(jnp.bfloat16)

    tags = tags_ref[...]
    factor = jnp.zeros(tags.shape, jnp.float32)
    for kind in range(norms_ref.shape[0]):
        factor = jnp.where(tags == kind, norms_ref[kind], factor)
    load_ket.wait()
    for slot in range(slot_count):
        scale = column_of(factor[slot:slot + 1, :])
        for h in range(batch // LANES):
            part = (slot, slice(None), slice(h * LANES, (h + 1) * LANES))
            ket[part] = (ket[part].astype(jnp.float32) * scale).astype(jnp.bfloat16)
    used = counts_ref[device]

    def stage_for(band):
        low = (band * column_size + column) * per_device
        chosen = jnp.int32(0)
        for slot in range(slot_count):
            target = targets_ref[device, slot]
            fits = (slot < used) & (target >= low) & (target < low + per_device)
            chosen = jnp.where(fits, jnp.int32(slot), chosen)
        return ket[chosen]

    landed[z] = stage_for(z)
    for d in range(1, n_rows):
        stage[d] = stage_for(lax.rem(z + d, n_rows))

    def ket_copy(d):
        return pltpu.make_async_remote_copy(
            src_ref=stage.at[d], dst_ref=landed.at[z], send_sem=ket_send.at[d],
            recv_sem=ket_recv.at[z], device_id={"rows": lax.rem(z + d, n_rows)},
            device_id_type=MESH)

    pl.semaphore_wait(barrier, n_rows + n_cols + n_sub - 3)

    def near(d):
        right = z < n_rows - 1 if d == 1 else False
        left = z > 0 if d == n_rows - 1 else False
        return jnp.logical_or(right, left)

    for d in range(1, n_rows):
        @pl.when(jnp.logical_not(near(d)))
        def _():
            ket_copy(d).start()

    def z_copy(src, dst, send, recv, q, dz):
        return pltpu.make_async_remote_copy(
            src_ref=src.at[q], dst_ref=dst.at[q], send_sem=send.at[q], recv_sem=recv.at[q],
            device_id={"rows": lax.rem(z + dz + n_rows, n_rows)}, device_id_type=MESH)

    def arrived(dst, sem):
        pltpu.make_async_remote_copy(
            src_ref=dst, dst_ref=dst, send_sem=sem, recv_sem=sem,
            device_id={"sub": lax.rem(s + 1, n_sub)}, device_id_type=MESH).wait_recv()

    load_vec.wait()
    piece = min(LANES, batch)
    in_piece = piece // z_rows
    for p in range(batch // piece):
        got = lax.dot_general(
            hot[p * piece:(p + 1) * piece, :], vec[...], (((1,), (1,)), ((), ())),
            preferred_element_type=jnp.float32).astype(jnp.bfloat16)
        got = got.reshape(in_piece, z_rows, width)
        own[p * in_piece:(p + 1) * in_piece] = got

        @pl.when(z == 0)
        def _():
            fwd_r[p * in_piece:(p + 1) * in_piece] = got
            for q in range(p * in_piece, (p + 1) * in_piece):
                z_copy(own, from_l, zr_send, l_recv, q, 1).start()

        @pl.when(z == n_rows - 1)
        def _():
            for q in range(p * in_piece, (p + 1) * in_piece):
                z_copy(own, from_r, zl_send, r_recv, q, -1).start()

    diag_col = column_of(diag_ref[...])
    row = lax.broadcasted_iota(jnp.int32, (rows_here, LANES), 0) + device * rows_here
    for h in range(batch // LANES):
        cut = slice(h * LANES, (h + 1) * LANES)
        share = jnp.sum(jnp.where(piv_ref[:, cut] == row, diag_col, 0.0), axis=0, keepdims=True)
        pd_z[n_rows, :, cut] = jnp.broadcast_to(share, (8, LANES))

    def pd_copies(src, dst, send, recv, name, here, count):
        return [pltpu.make_async_remote_copy(
            src_ref=src, dst_ref=dst.at[here], send_sem=send.at[d], recv_sem=recv.at[here],
            device_id={name: lax.rem(here + d, count)}, device_id_type=MESH)
            for d in range(1, count)]

    def pd_total(first, dst, recv, here, count):
        total = first[...]
        for d in range(1, count):
            other = lax.rem(here + d, count)
            arrived(dst.at[other], recv.at[other])
            total = total + dst[other]
        return total

    pdz = pd_copies(pd_z.at[n_rows], pd_z, pdz_send, pdz_recv, "rows", z, n_rows)
    pds = pd_copies(pd_own_s, pd_s, pds_send, pds_recv, "sub", s, n_sub)
    pdc = pd_copies(pd_own_c, pd_c, pdc_send, pdc_recv, "cols", x, n_cols)
    for c in pdz:
        c.start()

    load_prev.wait()
    prev_t[...] = jnp.transpose(prev[...].astype(jnp.float32))

    inner = (z > 0) & (z < n_rows - 1)
    tilt = jnp.where(inner, hop_lead * (2 * z - (n_rows - 1)), 0)
    wait_l = jnp.clip(tilt, 0, z_chunks)
    wait_r = jnp.clip(-tilt, 0, z_chunks)
    lag = jnp.maximum(wait_l, wait_r)
    most_lag = min(z_chunks, hop_lead * max(n_rows - 3, 0))

    def sub_copy(m, d):
        return pltpu.make_async_remote_copy(
            src_ref=sub_out.at[m, d], dst_ref=sub_in.at[m, s], send_sem=sub_send.at[m, d],
            recv_sem=sub_recv.at[m, s], device_id={"sub": lax.rem(s + d, n_sub)},
            device_id_type=MESH)

    def col_copy(m, d):
        return pltpu.make_async_remote_copy(
            src_ref=col_out.at[m, d], dst_ref=col_in.at[m, x], send_sem=col_send.at[m, d],
            recv_sem=col_recv.at[m, x], device_id={"cols": lax.rem(x + d, n_cols)},
            device_id_type=MESH)

    def block_dot(pivot_rows_t, col, sub):
        at = pl.multiple_of((col * n_sub + sub) * rows_here, LANES)
        return jnp.dot(
            pivot_rows_t, vec[:, pl.ds(at, rows_here)], preferred_element_type=jnp.float32)

    def multiply(m):
        rows = pl.ds(m * per_m, per_m)

        @pl.when(z < n_rows - 1)
        def _():
            pivot_t[rows] = fwd_r[rows] + from_r[rows]

        @pl.when(z == n_rows - 1)
        def _():
            pivot_t[rows] = fwd_r[rows]

        pt = pivot_t[rows].reshape(m_rows, width)
        for d in range(1, n_sub):
            for c in range(n_cols):
                sub_out[m, d, c] = block_dot(
                    pt, lax.rem(x + c, n_cols), lax.rem(s + d, n_sub))
            sub_copy(m, d).start()
        for c in range(1, n_cols):
            col_out[m, c] = block_dot(pt, lax.rem(x + c, n_cols), s)
        mine[m] = block_dot(pt, x, s)

    def reduce_chip(m):
        for d in range(1, n_sub):
            other = lax.rem(s + d, n_sub)
            arrived(sub_in.at[m, other], sub_recv.at[m, other])
        for c in range(1, n_cols):
            total = col_out[m, c]
            for d in range(1, n_sub):
                total = total + sub_in[m, lax.rem(s + d, n_sub), c]
            col_out[m, c] = total
            col_copy(m, c).start()
        total = mine[m]
        for d in range(1, n_sub):
            total = total + sub_in[m, lax.rem(s + d, n_sub), 0]
        mine[m] = total

    steps = most_lag + z_chunks + 1

    def step(t, carry):
        q_l, q_r, q_m = t - wait_l, t - wait_r, t - lag

        @pl.when((z > 0) & (q_l >= 0) & (q_l < z_chunks))
        def _():
            z_copy(fwd_r, from_l, zr_send, l_recv, q_l, 1).wait_recv()
            fwd_r[q_l] = from_l[q_l] + own[q_l]

            @pl.when(z < n_rows - 1)
            def _():
                z_copy(fwd_r, from_l, zr_send, l_recv, q_l, 1).start()

        @pl.when((z < n_rows - 1) & (q_r >= 0) & (q_r < z_chunks))
        def _():
            z_copy(fwd_l, from_r, zl_send, r_recv, q_r, -1).wait_recv()

            @pl.when(z > 0)
            def _():
                fwd_l[q_r] = from_r[q_r] + own[q_r]
                z_copy(fwd_l, from_r, zl_send, r_recv, q_r, -1).start()

        @pl.when(q_m == z_chunks - 1)
        def _():
            for d in (1, n_rows - 1):
                @pl.when(near(d))
                def _():
                    ket_copy(d).start()

        @pl.when((q_m >= per_m) & (q_m <= z_chunks) & (lax.rem(q_m, per_m) == 0))
        def _():
            reduce_chip(q_m // per_m - 1)

        @pl.when((q_m >= 0) & (q_m < z_chunks) & (lax.rem(q_m, per_m) == per_m - 1))
        def _():
            multiply(q_m // per_m)

        @pl.when(t == z_chunks // 2)
        def _():
            pd_own_s[...] = pd_total(pd_z.at[n_rows], pd_z, pdz_recv, z, n_rows)
            for c in pds:
                c.start()

        @pl.when(t == z_chunks - 1)
        def _():
            pd_own_c[...] = pd_total(pd_own_s, pd_s, pds_recv, s, n_sub)
            for c in pdc:
                c.start()

        return carry

    lax.fori_loop(0, steps, step, 0)

    pivot_diag = pd_total(pd_own_c, pd_c, pdc_recv, x, n_cols)
    inverse = 1.0 / jnp.sqrt(column_of(pivot_diag[0:1, :]))
    total_sq = jnp.zeros((1, rows_here), jnp.float32)
    per_t = max(LANES // m_rows, 1)
    for m in range(m_chunks):
        if m == m_chunks - 1:
            for d in range(1, n_rows):
                other = lax.rem(z + d, n_rows)
                arrived(landed.at[other], ket_recv.at[other])
            for place in range(per_device):
                block = device * per_device + place
                source = jnp.int32(0)
                for band in range(n_rows):
                    owner = band * column_size + column
                    for slot in range(slot_count):
                        fits = (slot < counts_ref[owner]) & (targets_ref[owner, slot] == block)
                        source = jnp.where(fits, jnp.int32(band), source)
                next_ref[place * block_rows:(place + 1) * block_rows, :] = landed[source]
        total = mine[m]
        for c in range(1, n_cols):
            other = lax.rem(x + c, n_cols)
            arrived(col_in.at[m, other], col_recv.at[m, other])
            total = total + col_in[m, other]
        rows = slice(m * m_rows, (m + 1) * m_rows)
        for h in range(rows_here // LANES):
            cut = slice(h * LANES, (h + 1) * LANES)
            scaled_t[rows, cut] = (prev_t[rows, cut] - total[:, cut]) * inverse[rows, :]
        scaled = scaled_t[rows, :]
        total_sq = total_sq + jnp.sum(scaled * scaled, axis=0, keepdims=True)
        if (m + 1) % per_t == 0:
            done = slice((m + 1 - per_t) * m_rows, (m + 1) * m_rows)
            new_ref[:, done] = jnp.transpose(scaled_t[done, :]).astype(jnp.bfloat16)
    diag_out_ref[...] = diag_ref[...] - total_sq

    for c in pdz + pds + pdc:
        c.wait_send()
    for d in range(1, n_rows):
        ket_copy(d).wait_send()

    @pl.when(z < n_rows - 1)
    def _():
        for q in range(z_chunks):
            z_copy(own, from_l, zr_send, l_recv, q, 1).wait_send()

    @pl.when(z > 0)
    def _():
        for q in range(z_chunks):
            z_copy(own, from_r, zl_send, r_recv, q, -1).wait_send()

    for m in range(m_chunks):
        for d in range(1, n_sub):
            sub_copy(m, d).wait_send()
        for c in range(1, n_cols):
            col_copy(m, c).wait_send()


def body(mesh_sizes, vectors, previous, pivots, diagonal, ket_blocks, tags, targets, counts, norms):
    n_rows, n_cols, n_sub = mesh_sizes
    width, band_rows = vectors.shape
    rows_here, batch = previous.shape
    slot_count, block_rows, _ = ket_blocks.shape
    z_chunks, m_chunks, hop_lead = 8, 4, 3
    z_rows, m_rows = batch // z_chunks, batch // m_chunks
    f32, bf16, dma = jnp.float32, jnp.bfloat16, pltpu.SemaphoreType.DMA
    line = pltpu.VMEM((z_chunks, z_rows, width), bf16)
    small = pltpu.VMEM((8, batch), f32)
    scratch = [
        pltpu.VMEM(vectors.shape, bf16), pltpu.VMEM(previous.shape, bf16),
        pltpu.VMEM(ket_blocks.shape, bf16), pltpu.VMEM((batch, band_rows), bf16),
        line, line, line, line, line, line,
        pltpu.VMEM((batch, rows_here), f32),
        pltpu.VMEM((m_chunks, n_sub, n_cols, m_rows, rows_here), f32),
        pltpu.VMEM((m_chunks, n_sub, n_cols, m_rows, rows_here), f32),
        pltpu.VMEM((m_chunks, m_rows, rows_here), f32),
        pltpu.VMEM((m_chunks, n_cols, m_rows, rows_here), f32),
        pltpu.VMEM((m_chunks, n_cols, m_rows, rows_here), f32),
        pltpu.VMEM((batch, rows_here), f32),
        pltpu.VMEM((n_rows, block_rows, batch), bf16),
        pltpu.VMEM((n_rows, block_rows, batch), bf16),
        pltpu.VMEM((n_rows + 1, 8, batch), f32), pltpu.VMEM((n_sub, 8, batch), f32),
        pltpu.VMEM((n_cols, 8, batch), f32), small, small,
        dma((3,)), dma((z_chunks,)), dma((z_chunks,)), dma((z_chunks,)), dma((z_chunks,)),
        dma((m_chunks, n_sub)), dma((m_chunks, n_sub)),
        dma((m_chunks, n_cols)), dma((m_chunks, n_cols)),
        dma((n_rows,)), dma((n_rows,)), dma((n_rows,)), dma((n_rows,)),
        dma((n_sub,)), dma((n_sub,)), dma((n_cols,)), dma((n_cols,)),
    ]
    hbm = pl.BlockSpec(memory_space=pl.ANY)
    vmem = pl.BlockSpec(memory_space=pltpu.VMEM)
    smem = pl.BlockSpec(memory_space=pltpu.SMEM)
    new_vectors, diag_out, next_columns = pl.pallas_call(
        functools.partial(kernel, (n_rows, n_cols, n_sub, hop_lead)),
        out_shape=(
            jax.ShapeDtypeStruct((rows_here, batch), bf16),
            jax.ShapeDtypeStruct((1, rows_here), f32),
            jax.ShapeDtypeStruct((rows_here, batch), bf16),
        ),
        in_specs=[hbm, hbm, vmem, vmem, hbm, vmem, smem, smem, smem],
        out_specs=(vmem, vmem, vmem),
        scratch_shapes=scratch,
        compiler_params=pltpu.CompilerParams(
            collective_id=0, has_side_effects=True, vmem_limit_bytes=48 * 1024 * 1024),
    )(
        vectors, previous, pivots.reshape(1, batch), diagonal.reshape(1, rows_here),
        ket_blocks, tags, targets, counts, norms,
    )
    return new_vectors, diag_out.reshape(rows_here), next_columns


def solution(mesh):
    sizes = tuple(mesh.shape[name] for name in ("rows", "cols", "sub"))
    return jax.shard_map(
        functools.partial(body, sizes),
        mesh=mesh,
        in_specs=(
            P(("cols", "sub"), ("groups", "rows")),
            P(("groups", "rows", "cols", "sub"), None),
            P("groups"),
            P(("groups", "rows", "cols", "sub")),
            P(("groups", "rows", "cols", "sub"), None, None),
            P(("groups", "rows", "cols", "sub"), None),
            P("groups", None),
            P("groups"),
            P(),
        ),
        out_specs=(
            P(("groups", "rows", "cols", "sub"), None),
            P(("groups", "rows", "cols", "sub")),
            P(("groups", "rows", "cols", "sub"), None),
        ),
        check_vma=False,
    )
```

time: 100 us -> 44.1 us (0.44)
  blocking collectives: 68.6 us -> 0 us
  Pallas kernels: 0 us -> 34 us
  between operations: 14.3 us -> 0.65 us
  other arithmetic: 3.79 us -> 0 us
  starting transfers between devices: 3.44 us -> 0 us
  matrix products: 2.14 us -> 0 us
  local copies, waits for them, and re-layouts: 7.74 us -> 9.24 us
    psum x2 -> x0, blocking collectives: 68.6 us -> none  [the longest x1 37.4 us: body(): pivot_rows = lax.psum(picked, 'rows').astype(jnp.bfloat16)]
    pallas_call x0 -> x1, Pallas kernels: none -> 34 us  [body(): pl.pallas_call(functools.partial(kernel, (n_rows, n_cols, n_sub, hop_lead...]
    unnamed x25 -> x20, local copies, waits for them, and re-layouts: 4.02 us -> 9.24 us
    all_to_all x1 -> x0, starting transfers between devices: 3.4 us -> none  [body(): lax.all_to_all(outgoing, 'rows', split_axis=0, concat_axis=0, tiled=True)]
    gather x3 -> x0, local copies, waits for them, and re-layouts: 2.39 us -> none  [the longest x1 1.19 us: body(): taken = jnp.take(stored_vectors, clamped, axis=1).astype(jnp.float32)]
    dot_general x3 -> x0, matrix products: 2.14 us -> none  [the longest x1 1.57 us: body(): lax.dot_general(stored_vectors, pivot_rows, (((0,), (0,)), ((), ())), pre...]
    reduce_sum x5 -> x0, other arithmetic: 1.68 us -> none  [the longest x1 1.08 us: body(): diag_out = diagonal - jnp.sum(scaled * scaled, axis=1)]
  transfers between devices with their start and end apart: 2 -> 0, of which waited for: 0 -> 0; matrix products, arithmetic and copies ran while one was open for 6% -> 0% of each run, Pallas kernels for 0% -> 0%
where the time goes in v1:
time: 44.1 us; the launch traced here: 43.8 us
  Pallas kernels  34 us (77%)
  local copies, waits for them, and re-layouts  9.24 us (21%)
  between operations  0.65 us (1%)
    pallas_call x1, Pallas kernels, body(): pl.pallas_call(functools.partial(kernel, (n_rows, n_cols, n_sub, hop_lead...  34 us
    unnamed x20, local copies, waits for them, and re-layouts  9.24 us

profile of v1, /device:TPU:0, one launch (start us, length us, event | category | flops | bytes accessed | tf_op | source)
XLA Modules:
  0.0 43.8 jit_solution(12296307395487842724)
XLA Ops:
  0.6 0.8 %copy.12.targets_ref = s32[16,4]{1,0:T(8,128)S(1)} copy(s32[16,4]{0,1:T(4,128)} %param.15) | data formatting | bytes 512 | tf_op args[6]
  1.4 0.0 copy-start
  1.4 1.4 %copy-done = bf16[768,1024]{1,0:T(8,128)(2,1)S(1)} copy-done((bf16[768,1024]{1,0:T(8,128)(2,1)S(1)}, bf16[768,1024]{1,0:T(8,128)(2,1)}, u32[]{:S(2)}) %copy-start) | copy-done | bytes 1572888
  2.8 0.0 copy-start.1
  2.8 0.9 %copy-done.1 = bf16[4,128,256]{2,1,0:T(8,128)(2,1)S(1)} copy-done((bf16[4,128,256]{2,1,0:T(8,128)(2,1)S(1)}, bf16[4,128,256]{2,1,0:T(8,128)(2,1)}, u32[]{:S(2)}) %copy-start.1) | copy-done | bytes 262168
  3.7 0.0 copy-start.2
  3.8 0.9 %copy-done.2 = bf16[256,256]{1,0:T(8,128)(2,1)S(1)} copy-done((bf16[256,256]{1,0:T(8,128)(2,1)S(1)}, bf16[256,256]{1,0:T(8,128)(2,1)}, u32[]{:S(2)}) %copy-start.2) | copy-done | bytes 131096
  4.7 0.0 copy-start.3
  4.7 0.7 %copy-done.3 = s32[4,128]{1,0:T(4,128)S(1)} copy-done((s32[4,128]{1,0:T(4,128)S(1)}, s32[4,128]{1,0:T(4,128)}, u32[]{:S(2)}) %copy-start.3) | copy-done | bytes 2072
  5.3 0.0 copy-start.4
  5.3 0.7 %copy-done.4 = s32[256]{0:T(256)S(1)} copy-done((s32[256]{0:T(256)S(1)}, s32[256]{0:T(256)}, u32[]{:S(2)}) %copy-start.4) | copy-done | bytes 1048
  6.0 0.0 copy-start.5
  6.0 0.7 %copy-done.5 = f32[256]{0:T(256)S(1)} copy-done((f32[256]{0:T(256)S(1)}, f32[256]{0:T(256)}, u32[]{:S(2)}) %copy-start.5) | copy-done | bytes 1048
  6.7 0.0 copy-start.6
  6.7 0.7 %copy-done.6 = s32[16]{0:T(128)S(1)} copy-done((s32[16]{0:T(128)S(1)}, s32[16]{0:T(128)}, u32[]{:S(2)}) %copy-start.6) | copy-done | bytes 88
  7.3 0.0 copy-start.7
  7.4 0.7 %copy-done.7 = f32[4]{0:T(128)S(1)} copy-done((f32[4]{0:T(128)S(1)}, f32[4]{0:T(128)}, u32[]{:S(2)}) %copy-start.7) | copy-done | bytes 40
  8.0 34.0 %shard_map.112 = (bf16[256,256]{1,0:T(8,128)(2,1)S(1)}, f32[1,256]{1,0:T(1,128)S(1)}, bf16[256,256]{1,0:T(8,128)(2,1)S(1)}) custom-call(bf16[768,1024]{1,0:T(8,128)(2,1)S(1)} %copy-done, bf16[256,256]{1,0:T(8,128)(2,1)S(1)} %copy-done.2, s32[1,256]{1,0:T(1,128)S(1)} %bitcast.3, f32[1,256]{1,0:T(1,128)S(1)} %bitcast.4, bf16[4,128,256]{2,1,0:T(8,128)(2,1)S(1)} %copy-done.1, ...), custom_call_target="tpu_custom_call" | custom-call | tf_op jit(solution)/shard_map/pallas_call | solution.py:369
  42.0 0.7 %copy.16 = bf16[256,256]{1,0:T(8,128)(2,1)} copy(bf16[256,256]{1,0:T(8,128)(2,1)S(1)} %get-tuple-element.12) | data formatting | bytes 262144
  42.6 0.6 %copy.17 = f32[256]{0:T(256)} copy(f32[256]{0:T(256)S(1)} %bitcast.5) | data formatting | bytes 2048
  43.2 0.7 %copy.18 = bf16[256,256]{1,0:T(8,128)(2,1)} copy(bf16[256,256]{1,0:T(8,128)(2,1)S(1)} %get-tuple-element.14) | data formatting | bytes 262144
Async XLA Ops:
  1.4 1.4 %copy-start = (bf16[768,1024]{1,0:T(8,128)(2,1)S(1)}, bf16[768,1024]{1,0:T(8,128)(2,1)}, u32[]{:S(2)}) copy-start(bf16[768,1024]{1,0:T(8,128)(2,1)} %vec_hbm.1) | copy-start | bytes 4718596
  2.8 0.9 %copy-start.1 = (bf16[4,128,256]{2,1,0:T(8,128)(2,1)S(1)}, bf16[4,128,256]{2,1,0:T(8,128)(2,1)}, u32[]{:S(2)}) copy-start(bf16[4,128,256]{2,1,0:T(8,128)(2,1)} %ket_hbm.1) | copy-start | bytes 786436
  3.7 0.9 %copy-start.2 = (bf16[256,256]{1,0:T(8,128)(2,1)S(1)}, bf16[256,256]{1,0:T(8,128)(2,1)}, u32[]{:S(2)}) copy-start(bf16[256,256]{1,0:T(8,128)(2,1)} %prev_hbm.1) | copy-start | bytes 393220
  4.7 0.7 %copy-start.3 = (s32[4,128]{1,0:T(4,128)S(1)}, s32[4,128]{1,0:T(4,128)}, u32[]{:S(2)}) copy-start(s32[4,128]{1,0:T(4,128)} %tags_ref.1) | copy-start | bytes 6148
  5.3 0.7 %copy-start.4 = (s32[256]{0:T(256)S(1)}, s32[256]{0:T(256)}, u32[]{:S(2)}) copy-start(s32[256]{0:T(256)} %param.11) | copy-start | bytes 3076
  6.0 0.7 %copy-start.5 = (f32[256]{0:T(256)S(1)}, f32[256]{0:T(256)}, u32[]{:S(2)}) copy-start(f32[256]{0:T(256)} %param.12) | copy-start | bytes 3076
  6.7 0.7 %copy-start.6 = (s32[16]{0:T(128)S(1)}, s32[16]{0:T(128)}, u32[]{:S(2)}) copy-start(s32[16]{0:T(128)} %counts_ref.1) | copy-start | bytes 196
  7.3 0.7 %copy-start.7 = (f32[4]{0:T(128)S(1)}, f32[4]{0:T(128)}, u32[]{:S(2)}) copy-start(f32[4]{0:T(128)} %norms_ref.1) | copy-start | bytes 52

commit v2 on v1

--- a/solution.py
+++ b/solution.py
@@ -74,7 +74,7 @@
         low = (band * column_size + column) * per_device
         chosen = jnp.int32(0)
         for slot in range(slot_count):
-            target = targets_ref[device, slot]
+            target = targets_ref[slot, device]
             fits = (slot < used) & (target >= low) & (target < low + per_device)
             chosen = jnp.where(fits, jnp.int32(slot), chosen)
         return ket[chosen]
@@ -291,7 +291,7 @@
                 for band in range(n_rows):
                     owner = band * column_size + column
                     for slot in range(slot_count):
-                        fits = (slot < counts_ref[owner]) & (targets_ref[owner, slot] == block)
+                        fits = (slot < counts_ref[owner]) & (targets_ref[slot, owner] == block)
                         source = jnp.where(fits, jnp.int32(band), source)
                 next_ref[place * block_rows:(place + 1) * block_rows, :] = landed[source]
         total = mine[m]
@@ -377,10 +377,10 @@
         out_specs=(vmem, vmem, vmem),
         scratch_shapes=scratch,
         compiler_params=pltpu.CompilerParams(
-            collective_id=0, has_side_effects=True, vmem_limit_bytes=48 * 1024 * 1024),
+            collective_id=0, has_side_effects=True, vmem_limit_bytes=67043328),
     )(
         vectors, previous, pivots.reshape(1, batch), diagonal.reshape(1, rows_here),
-        ket_blocks, tags, targets, counts, norms,
+        ket_blocks, tags, targets.T, counts, norms,
     )
     return new_vectors, diag_out.reshape(rows_here), next_columns
 

time: 44.1 us -> 39.8 us (0.902)
  local copies, waits for them, and re-layouts: 9.24 us -> 4.37 us
  Pallas kernels: 34 us -> 34.5 us
    unnamed x20 -> x3, local copies, waits for them, and re-layouts: 9.24 us -> 4.37 us
    pallas_call x1, Pallas kernels: 34 us -> 34.5 us  [body(): pl.pallas_call(functools.partial(kernel, (n_rows, n_cols, n_sub, hop_lead...]
where the time goes in v2:
time: 39.8 us; the launch traced here: 39.6 us
  Pallas kernels  34.5 us (87%)
  local copies, waits for them, and re-layouts  4.37 us (11%)
  between operations  0.64 us (2%)
    pallas_call x1, Pallas kernels, body(): pl.pallas_call(functools.partial(kernel, (n_rows, n_cols, n_sub, hop_lead...  34.5 us
    unnamed x3, local copies, waits for them, and re-layouts  4.37 us

profile of v2, /device:TPU:0, one launch (start us, length us, event | category | flops | bytes accessed | tf_op | source)
XLA Modules:
  0.0 39.6 jit_solution(5862993385518097403)
XLA Ops:
  0.6 34.5 %shard_map.112 = (bf16[256,256]{1,0:T(8,128)(2,1)}, f32[1,256]{1,0:T(1,128)}, bf16[256,256]{1,0:T(8,128)(2,1)}) custom-call(bf16[768,1024]{1,0:T(8,128)(2,1)} %vec_hbm.1, bf16[256,256]{1,0:T(8,128)(2,1)} %prev_hbm.1, s32[1,256]{1,0:T(1,128)} %bitcast.5, f32[1,256]{1,0:T(1,128)} %bitcast.6, bf16[4,128,256]{2,1,0:T(8,128)(2,1)} %ket_hbm.1, s32[4,128]{1,0:T(4,128)} %tags_ref.1, ...), custom_call_target="tpu_custom_call" | custom-call | tf_op jit(solution)/shard_map/pallas_call | solution.py:369
  35.2 1.6 %copy.15 = bf16[256,256]{1,0:T(8,128)(2,1)} copy(bf16[256,256]{1,0:T(8,128)(2,1)} %get-tuple-element.12) | data formatting | bytes 262144
  36.8 1.2 %copy.16 = f32[256]{0:T(256)} copy(f32[256]{0:T(256)} %bitcast.7) | data formatting | bytes 2048
  38.0 1.6 %copy.17 = bf16[256,256]{1,0:T(8,128)(2,1)} copy(bf16[256,256]{1,0:T(8,128)(2,1)} %get-tuple-element.14) | data formatting | bytes 262144

commit v3 on v2

--- a/solution.py
+++ b/solution.py
@@ -58,6 +58,13 @@
         hot[:, t * LANES:(t + 1) * LANES] = (piv_col == lane + t * LANES).astype(
             jnp.float32).astype(jnp.bfloat16)
 
+    diag_col = column_of(diag_ref[...])
+    row = lax.broadcasted_iota(jnp.int32, (rows_here, LANES), 0) + device * rows_here
+    for h in range(batch // LANES):
+        cut = slice(h * LANES, (h + 1) * LANES)
+        share = jnp.sum(jnp.where(piv_ref[:, cut] == row, diag_col, 0.0), axis=0, keepdims=True)
+        pd_z[n_rows, :, cut] = jnp.broadcast_to(share, (8, LANES))
+
     tags = tags_ref[...]
     factor = jnp.zeros(tags.shape, jnp.float32)
     for kind in range(norms_ref.shape[0]):
@@ -91,14 +98,23 @@
 
     pl.semaphore_wait(barrier, n_rows + n_cols + n_sub - 3)
 
-    def near(d):
-        right = z < n_rows - 1 if d == 1 else False
-        left = z > 0 if d == n_rows - 1 else False
-        return jnp.logical_or(right, left)
-
-    for d in range(1, n_rows):
-        @pl.when(jnp.logical_not(near(d)))
-        def _():
+    def pd_copies(src, dst, send, recv, name, here, count):
+        return [pltpu.make_async_remote_copy(
+            src_ref=src, dst_ref=dst.at[here], send_sem=send.at[d], recv_sem=recv.at[here],
+            device_id={name: lax.rem(here + d, count)}, device_id_type=MESH)
+            for d in range(1, count)]
+
+    pdz = pd_copies(pd_z.at[n_rows], pd_z, pdz_send, pdz_recv, "rows", z, n_rows)
+    pds = pd_copies(pd_own_s, pd_s, pds_send, pds_recv, "sub", s, n_sub)
+    pdc = pd_copies(pd_own_c, pd_c, pdc_send, pdc_recv, "cols", x, n_cols)
+    for c in pdz:
+        c.start()
+
+    inner = (z > 0) & (z < n_rows - 1)
+
+    @pl.when(inner)
+    def _():
+        for d in range(1, n_rows):
             ket_copy(d).start()
 
     def z_copy(src, dst, send, recv, q, dz):
@@ -132,19 +148,6 @@
             for q in range(p * in_piece, (p + 1) * in_piece):
                 z_copy(own, from_r, zl_send, r_recv, q, -1).start()
 
-    diag_col = column_of(diag_ref[...])
-    row = lax.broadcasted_iota(jnp.int32, (rows_here, LANES), 0) + device * rows_here
-    for h in range(batch // LANES):
-        cut = slice(h * LANES, (h + 1) * LANES)
-        share = jnp.sum(jnp.where(piv_ref[:, cut] == row, diag_col, 0.0), axis=0, keepdims=True)
-        pd_z[n_rows, :, cut] = jnp.broadcast_to(share, (8, LANES))
-
-    def pd_copies(src, dst, send, recv, name, here, count):
-        return [pltpu.make_async_remote_copy(
-            src_ref=src, dst_ref=dst.at[here], send_sem=send.at[d], recv_sem=recv.at[here],
-            device_id={name: lax.rem(here + d, count)}, device_id_type=MESH)
-            for d in range(1, count)]
-
     def pd_total(first, dst, recv, here, count):
         total = first[...]
         for d in range(1, count):
@@ -153,16 +156,9 @@
             total = total + dst[other]
         return total
 
-    pdz = pd_copies(pd_z.at[n_rows], pd_z, pdz_send, pdz_recv, "rows", z, n_rows)
-    pds = pd_copies(pd_own_s, pd_s, pds_send, pds_recv, "sub", s, n_sub)
-    pdc = pd_copies(pd_own_c, pd_c, pdc_send, pdc_recv, "cols", x, n_cols)
-    for c in pdz:
-        c.start()
-
     load_prev.wait()
     prev_t[...] = jnp.transpose(prev[...].astype(jnp.float32))
 
-    inner = (z > 0) & (z < n_rows - 1)
     tilt = jnp.where(inner, hop_lead * (2 * z - (n_rows - 1)), 0)
     wait_l = jnp.clip(tilt, 0, z_chunks)
     wait_r = jnp.clip(-tilt, 0, z_chunks)
@@ -245,12 +241,10 @@
                 fwd_l[q_r] = from_r[q_r] + own[q_r]
                 z_copy(fwd_l, from_r, zl_send, r_recv, q_r, -1).start()
 
-        @pl.when(q_m == z_chunks - 1)
-        def _():
-            for d in (1, n_rows - 1):
-                @pl.when(near(d))
-                def _():
-                    ket_copy(d).start()
+        @pl.when(jnp.logical_not(inner) & (q_m == z_chunks - 2))
+        def _():
+            for d in range(1, n_rows):
+                ket_copy(d).start()
 
         @pl.when((q_m >= per_m) & (q_m <= z_chunks) & (lax.rem(q_m, per_m) == 0))
         def _():
@@ -369,15 +363,15 @@
     new_vectors, diag_out, next_columns = pl.pallas_call(
         functools.partial(kernel, (n_rows, n_cols, n_sub, hop_lead)),
         out_shape=(
-            jax.ShapeDtypeStruct((rows_here, batch), bf16),
-            jax.ShapeDtypeStruct((1, rows_here), f32),
-            jax.ShapeDtypeStruct((rows_here, batch), bf16),
+            pltpu.VMEM((rows_here, batch), bf16),
+            pltpu.VMEM((1, rows_here), f32),
+            pltpu.VMEM((rows_here, batch), bf16),
         ),
         in_specs=[hbm, hbm, vmem, vmem, hbm, vmem, smem, smem, smem],
         out_specs=(vmem, vmem, vmem),
         scratch_shapes=scratch,
         compiler_params=pltpu.CompilerParams(
-            collective_id=0, has_side_effects=True, vmem_limit_bytes=67043328),
+            collective_id=0, has_side_effects=True, vmem_limit_bytes=63 * 1024 * 1024),
     )(
         vectors, previous, pivots.reshape(1, batch), diagonal.reshape(1, rows_here),
         ket_blocks, tags, targets.T, counts, norms,

time: 39.8 us -> 33.3 us (0.84)
  Pallas kernels: 34.5 us -> 30.6 us
  local copies, waits for them, and re-layouts: 4.37 us -> 1.88 us
    pallas_call x1, Pallas kernels: 34.5 us -> 30.6 us  [body(): pl.pallas_call(functools.partial(kernel, (n_rows, n_cols, n_sub, hop_lead...]
    unnamed x3, local copies, waits for them, and re-layouts: 4.37 us -> 1.88 us
where the time goes in v3:
time: 33.3 us; the launch traced here: 33.2 us
  Pallas kernels  30.6 us (92%)
  local copies, waits for them, and re-layouts  1.88 us (6%)
  between operations  0.64 us (2%)
    pallas_call x1, Pallas kernels, body(): pl.pallas_call(functools.partial(kernel, (n_rows, n_cols, n_sub, hop_lead...  30.6 us
    unnamed x3, local copies, waits for them, and re-layouts  1.88 us

profile of v3, /device:TPU:0, one launch (start us, length us, event | category | flops | bytes accessed | tf_op | source)
XLA Modules:
  0.0 33.2 jit_solution(7841059162868383684)
XLA Ops:
  0.6 30.6 %shard_map.112 = (bf16[256,256]{1,0:T(8,128)(2,1)S(1)}, f32[1,256]{1,0:T(1,128)S(1)}, bf16[256,256]{1,0:T(8,128)(2,1)S(1)}) custom-call(bf16[768,1024]{1,0:T(8,128)(2,1)} %vec_hbm.1, bf16[256,256]{1,0:T(8,128)(2,1)} %prev_hbm.1, s32[1,256]{1,0:T(1,128)} %bitcast.6, f32[1,256]{1,0:T(1,128)} %bitcast.7, bf16[4,128,256]{2,1,0:T(8,128)(2,1)} %ket_hbm.1, ...), custom_call_target="tpu_custom_call" | custom-call | tf_op jit(solution)/shard_map/pallas_call | solution.py:363
  31.3 0.7 %copy.15 = bf16[256,256]{1,0:T(8,128)(2,1)} copy(bf16[256,256]{1,0:T(8,128)(2,1)S(1)} %get-tuple-element.9) | data formatting | bytes 262144
  31.9 0.6 %copy.16 = f32[256]{0:T(256)} copy(f32[256]{0:T(256)S(1)} %bitcast.4) | data formatting | bytes 2048
  32.5 0.7 %copy.17 = bf16[256,256]{1,0:T(8,128)(2,1)} copy(bf16[256,256]{1,0:T(8,128)(2,1)S(1)} %get-tuple-element.11) | data formatting | bytes 262144
